TPU v7x, 32 devices: a whole 2x2x4 slice. The times are simulated.
32 devices in a mesh: batch: 4 (over y, core), tensor: 2 (over x), latent: 4 (over z).
Axes of the slice: x: 2, y: 2, z: 4, core: 2. Of those that a mesh axis runs over, the one named last changes fastest.
Arguments:
- residual: bfloat16 [1024, 3584], P('batch', ('tensor', 'latent')), may hold values from -6 to 6
- target: bfloat16 [1024, 3584], P('batch', ('tensor', 'latent')), may hold values from -6 to 6
- encoder_weight: bfloat16 [3584, 32768], P(None, ('tensor', 'latent')), may hold values from -0.09375 to 0.09375
- encoder_bias: bfloat16 [32768], P(('tensor', 'latent')), may hold values from -0.59765625 to 0.29882812
- decoder_weight: bfloat16 [32768, 3584], P(('tensor', 'latent')), may hold values from -0.0625 to 0.0625
- decoder_bias: bfloat16 [3584], replicated, may hold values from -3 to 3
- first_gain: bfloat16 [3584], replicated, may hold values from 0.5 to 1.5
- second_gain: bfloat16 [3584], replicated, may hold values from 0.5 to 1.5
- gate_weight: bfloat16 [3584, 7168], P(None, ('tensor', 'latent')), may hold values from -0.09375 to 0.09375
- up_weight: bfloat16 [3584, 7168], P(None, ('tensor', 'latent')), may hold values from -0.09375 to 0.09375
- down_weight: bfloat16 [7168, 3584], P(('tensor', 'latent')), may hold values from -0.09375 to 0.09375
Outputs:
- encoder_grad: bfloat16 [3584, 32768], P('batch', ('tensor', 'latent'))
- decoder_grad: bfloat16 [32768, 3584], P(('tensor', 'latent'), 'batch')
All inputs are finite; a program needn't handle non-finite values.
Results may differ from a plain program's by a relative error of at most 0.012.
The roundings to bfloat16 on the way count: a program that leaves them out, or rounds other values in their place, can miss the bound.
Values may be sent and summed in bfloat16 or wider, within the bound.
A program may use at most 192 MiB of HBM per device.

v0:
```python
import jax
import jax.numpy as jnp
from jax import lax
from jax.sharding import PartitionSpec as P

epsilon = 1e-06


def per_device(
    residual,
    target,
    encoder_weight,
    encoder_bias,
    decoder_weight,
    decoder_bias,
    first_gain,
    second_gain,
    gate_weight,
    up_weight,
    down_weight,
):
    f32 = jnp.float32
    bf16 = jnp.bfloat16
    contract_last = (((1,), (1,)), ((), ()))
    contract_first = (((0,), (0,)), ((), ()))
    share_width = residual.shape[1]
    model_width = share_width * lax.axis_size(("tensor", "latent"))
    offset = lax.axis_index(("tensor", "latent")) * share_width
    token_count = residual.shape[0] * lax.axis_size("batch")
    bias_share = lax.dynamic_slice_in_dim(decoder_bias.astype(f32), offset, share_width)
    first_share = lax.dynamic_slice_in_dim(first_gain.astype(f32), offset, share_width)
    second_share = lax.dynamic_slice_in_dim(second_gain.astype(f32), offset, share_width)
    centered_share = (residual.astype(f32) - bias_share).astype(bf16)
    centered = lax.all_gather(centered_share, ("tensor", "latent"), axis=1, tiled=True)
    preact = jnp.dot(centered, encoder_weight, preferred_element_type=f32) + encoder_bias.astype(
        f32
    )
    latents = jnp.maximum(preact, 0.0).astype(bf16)
    partial_recon = jnp.dot(latents, decoder_weight, preferred_element_type=f32)
    recon_full = lax.psum(partial_recon.astype(jnp.bfloat16), ("tensor", "latent")).astype(
        jnp.float32
    ) + decoder_bias.astype(f32)
    scale_in = lax.rsqrt(
        jnp.sum(recon_full * recon_full, axis=1, keepdims=True) / model_width + epsilon
    )
    normed_input = (recon_full * scale_in * first_gain.astype(f32)).astype(bf16)
    recon = lax.dynamic_slice_in_dim(recon_full, offset, share_width, 1)
    gate_value = jnp.dot(normed_input, gate_weight, preferred_element_type=f32)
    up_value = jnp.dot(normed_input, up_weight, preferred_element_type=f32)
    gelu_value, gelu_back = jax.vjp(lambda v: jax.nn.gelu(v, approximate=True), gate_value)
    hidden = (gelu_value * up_value).astype(bf16)
    partial_out = jnp.dot(hidden, down_weight, preferred_element_type=f32)
    output = lax.psum_scatter(
        partial_out.astype(jnp.bfloat16), ("tensor", "latent"), scatter_dimension=1, tiled=True
    ).astype(jnp.float32)
    out_squares = lax.psum(jnp.sum(output * output, axis=1), ("tensor", "latent"))
    scale_out = lax.rsqrt(out_squares[:, None] / model_width + epsilon)
    normed_out = output * scale_out
    result = recon + normed_out * second_share
    grad_result = 2.0 * (result - target.astype(f32)) / token_count
    grad_normed = grad_result * second_share
    inner_out = (
        lax.psum(jnp.sum(grad_normed * normed_out, axis=1), ("tensor", "latent")) / model_width
    )
    grad_share = (scale_out * (grad_normed - normed_out * inner_out[:, None])).astype(bf16)
    grad_output = lax.all_gather(grad_share, ("tensor", "latent"), axis=1, tiled=True)
    grad_hidden = lax.dot_general(
        grad_output, down_weight, contract_last, preferred_element_type=f32
    )
    grad_gate = gelu_back(grad_hidden * up_value)[0].astype(bf16)
    grad_up = (grad_hidden * gelu_value).astype(bf16)
    partial_input = lax.dot_general(
        grad_gate, gate_weight, contract_last, preferred_element_type=f32
    )
    partial_input = partial_input + lax.dot_general(
        grad_up, up_weight, contract_last, preferred_element_type=f32
    )
    grad_normed_in = lax.psum_scatter(
        partial_input.astype(jnp.bfloat16), ("tensor", "latent"), scatter_dimension=1, tiled=True
    ).astype(jnp.float32)
    unit = recon * scale_in
    grad_unit = grad_normed_in * first_share
    inner_in = lax.psum(jnp.sum(grad_unit * unit, axis=1), ("tensor", "latent")) / model_width
    recon_share = (grad_result + scale_in * (grad_unit - unit * inner_in[:, None])).astype(bf16)
    grad_recon = lax.all_gather(recon_share, ("tensor", "latent"), axis=1, tiled=True)
    grad_latent = lax.dot_general(
        grad_recon, decoder_weight, contract_last, preferred_element_type=f32
    )
    grad_preact = jnp.where(preact > 0, grad_latent, 0.0).astype(bf16)
    centered_block, recon_block = (
        lax.all_to_all(centered, "batch", split_axis=1, concat_axis=0, tiled=True),
        lax.all_to_all(grad_recon, "batch", split_axis=1, concat_axis=0, tiled=True),
    )
    latents_all, preact_all = (
        lax.all_gather(latents, "batch", axis=0, tiled=True),
        lax.all_gather(grad_preact, "batch", axis=0, tiled=True),
    )
    encoder_grad = lax.dot_general(
        centered_block, preact_all, contract_first, preferred_element_type=f32
    )
    decoder_grad = lax.dot_general(
        latents_all, recon_block, contract_first, preferred_element_type=f32
    )
    return (encoder_grad.astype(bf16), decoder_grad.astype(bf16))


def solution(mesh):
    in_specs = (
        P("batch", ("tensor", "latent")),
        P("batch", ("tensor", "latent")),
        P(None, ("tensor", "latent")),
        P(("tensor", "latent")),
        P(("tensor", "latent"), None),
        P(),
        P(),
        P(),
        P(None, ("tensor", "latent")),
        P(None, ("tensor", "latent")),
        P(("tensor", "latent"), None),
    )
    out_specs = (P("batch", ("tensor", "latent")), P(("tensor", "latent"), "batch"))
    return jax.shard_map(
        per_device, mesh=mesh, in_specs=in_specs, out_specs=out_specs, check_vma=False
    )
```

profile of v0, /device:TPU:0, one launch (start us, length us, event | category | flops | bytes accessed | tf_op | source)
XLA Modules:
  0.0 670.3 jit_solution(1007464066563289429)
XLA Ops:
  7.2 0.0 all-gather.6.cloned.1.call-start
  7.2 0.8 dynamic_slice.12
  8.0 1.8 subtract_convert_fusion
  9.7 0.0 all-gather.6.cloned.1.call-update
  9.8 0.0 all-reduce.2.cloned.1.call-start
  9.8 0.7 convert_element_type.74
  10.5 49.3 %all-gather.6.cloned.1.call-done = bf16[256,3584]{0,1:T(8,128)(2,1)} async-done(((bf16[256,448]{0,1:T(8,128)(2,1)}), bf16[256,3584]{0,1:T(8,128)(2,1)}) %all-gather.6.cloned.1.call-update) | async-done | bytes 1835024 | tf_op jit(solution)/shard_map/all_gather | solution.py:34
  59.8 15.2 %maximum_convert_fusion = (bf16[256,4096]{1,0:T(8,128)(2,1)S(1)}, f32[256,4096]{1,0:T(8,128)}) fusion(f32[4096]{0:T(1024)S(1)} %convert_element_type.74, bf16[256,3584]{0,1:T(8,128)(2,1)} %all-gather.6.cloned.1.call-done, bf16[3584,4096]{1,0:T(8,128)(2,1)} %param.13), kind=kOutput, calls=%fused_computation.11 | convolution fusion | flops 7519338496 | bytes 37502976 | tf_op jit(solution)/shard_map/dot_general | solution.py:35
  75.0 15.5 %convolution_convert_fusion.2 = bf16[256,3584]{1,0:T(8,128)(2,1)} fusion(bf16[256,4096]{1,0:T(8,128)(2,1)S(1)} %get-tuple-element.4, bf16[4096,3584]{1,0:T(8,128)(2,1)} %param.15), kind=kOutput, calls=%fused_computation.5 | convolution fusion | flops 7517110272 | bytes 33292288 | tf_op jit(solution)/shard_map/dot_general | solution.py:39
  90.5 0.0 all-reduce.2.cloned.1.call-update
  90.5 0.2 reduce-scatter.7.cloned.1.call-start
  90.7 94.5 %all-reduce.2.cloned.1.call-done = bf16[256,3584]{1,0:T(8,128)(2,1)} async-done(((bf16[256,3584]{1,0:T(8,128)(2,1)}), bf16[256,3584]{1,0:T(8,128)(2,1)}) %all-reduce.2.cloned.1.call-update) | async-done | bytes 1835024 | tf_op jit(solution)/shard_map/psum | solution.py:40
  185.2 4.0 convert_add_fusion
  189.2 0.0 slice-start.4
  189.2 5.6 fusion.30
  194.8 0.0 slice-done
  194.9 0.0 slice-start.5
  194.9 2.1 fusion.29
  197.1 0.0 copy-start.4
  197.1 4.3 fusion.2
  201.4 0.0 reduce-scatter.7.cloned.1.call-update
  201.4 0.0 all-gather.8.cloned.1.call-start
  201.4 0.1 copy.36
  201.6 0.8 broadcast_multiply_fusion
  202.4 0.8 dynamic-slice_convert_fusion
  203.1 64.5 %reduce-scatter.7.cloned.1.call-done = bf16[448,256]{1,0:T(8,128)(2,1)} async-done(((bf16[3584,256]{1,0:T(8,128)(2,1)}), bf16[448,256]{1,0:T(8,128)(2,1)}) %reduce-scatter.7.cloned.1.call-update) | async-done | bytes 229392
  267.7 1.1 copy.42
  268.7 0.1 fusion.20
  268.9 19.4 %psum.29 = f32[256]{0:T(256)S(1)} all-reduce(f32[256]{0:T(256)S(1)} %fusion.20), channel_id=1, replica_groups=mesh['batch'=4,'tensor'=2,'latent'=4] {'tensor','latent'}, use_global_device_ids=true, to_apply=%region_4.0 | all-reduce | flops 256 | bytes 2048 | tf_op jit(solution)/shard_map/psum | solution.py:56
  288.3 1.4 fusion.16
  289.7 17.2 %psum.30 = f32[256]{0:T(256)S(1)} all-reduce(f32[256]{0:T(256)S(1)} %fusion.16), channel_id=1, replica_groups=mesh['batch'=4,'tensor'=2,'latent'=4] {'tensor','latent'}, use_global_device_ids=true, to_apply=%region_6.0 | all-reduce | flops 256 | bytes 2048 | tf_op jit(solution)/shard_map/psum | solution.py:63
  307.0 1.4 fusion.19
  308.4 0.9 copy.37
  309.2 0.0 all-gather.8.cloned.1.call-update
  309.2 0.3 reduce-scatter.9.cloned.1.call-start
  309.5 45.8 %all-gather.8.cloned.1.call-done = bf16[256,3584]{0,1:T(8,128)(2,1)} async-done(((bf16[256,448]{0,1:T(8,128)(2,1)}), bf16[256,3584]{0,1:T(8,128)(2,1)}) %all-gather.8.cloned.1.call-update) | async-done | bytes 1835024 | tf_op jit(solution)/shard_map/all_gather | solution.py:66
  355.3 5.6 fusion.45
  361.0 0.0 slice-start.3
  361.0 5.4 fusion.21
  366.5 3.6 fusion.3
  370.1 0.0 reduce-scatter.9.cloned.1.call-update
  370.1 0.0 all-gather.10.cloned.1.call-start
  370.2 0.1 dynamic_slice.15
  370.3 65.2 %reduce-scatter.9.cloned.1.call-done = bf16[448,256]{1,0:T(8,128)(2,1)} async-done(((bf16[3584,256]{1,0:T(8,128)(2,1)}), bf16[448,256]{1,0:T(8,128)(2,1)}) %reduce-scatter.9.cloned.1.call-update) | async-done | bytes 229392
  435.5 1.1 copy.44
  436.6 1.4 multiply_reduce_fusion.1
  438.0 19.3 %psum.31 = f32[256]{0:T(256)S(1)} all-reduce(f32[256]{0:T(256)S(1)} %multiply_reduce_fusion.1), channel_id=1, replica_groups=mesh['batch'=4,'tensor'=2,'latent'=4] {'tensor','latent'}, use_global_device_ids=true, to_apply=%region_9.0 | all-reduce | flops 256 | bytes 2048 | tf_op jit(solution)/shard_map/psum | solution.py:83
  457.3 1.5 add_convert_fusion
  458.8 0.8 copy.39
  459.7 0.0 all-gather.10.cloned.1.call-update
  459.7 0.0 all-gather.14.cloned.1.call-start
  459.7 0.7 all-gather.14.cloned.1.call-update
  460.4 0.0 all-gather.12.cloned.1.call-start
  460.5 44.0 %all-gather.10.cloned.1.call-done = bf16[256,3584]{0,1:T(8,128)(2,1)} async-done(((bf16[256,448]{0,1:T(8,128)(2,1)}), bf16[256,3584]{0,1:T(8,128)(2,1)}) %all-gather.10.cloned.1.call-update) | async-done | bytes 1835024 | tf_op jit(solution)/shard_map/all_gather | solution.py:85
  504.5 18.3 %fusion = bf16[256,4096]{1,0:T(8,128)(2,1)} fusion(bf16[256,3584]{0,1:T(8,128)(2,1)} %all-gather.10.cloned.1.call-done, bf16[4096,3584]{1,0:T(8,128)(2,1)} %param.15, f32[256,4096]{1,0:T(8,128)} %get-tuple-element.5), kind=kOutput, calls=%fused_computation.6 | convolution fusion | flops 7519338496 | bytes 37486592 | tf_op jit(solution)/shard_map/dot_general | solution.py:86
  522.8 0.0 all-gather.12.cloned.1.call-update
  522.8 46.2 %all_to_all.38 = bf16[256,4,896]{0,2,1:T(8,128)(2,1)} all-to-all(bf16[256,4,896]{0,2,1:T(8,128)(2,1)S(1)} %bitcast.35), channel_id=1, replica_groups=mesh['batch'=4,'tensor'=2,'latent'=4] {'batch'}, dimensions={1} | all-to-all | bytes 3670016 | tf_op jit(solution)/shard_map/all_to_all | solution.py:91
  569.0 3.8 all-to-all-start.1
  572.9 3.6 copy.34
  576.5 24.1 %all-to-all-done.1 = bf16[256,4,896]{0,2,1:T(8,128)(2,1)S(1)} async-done(((bf16[256,4,896]{0,2,1:T(8,128)(2,1)}), bf16[256,4,896]{0,2,1:T(8,128)(2,1)S(1)}, u32[]{:S(2)}, u32[]{:S(2)}) %all-to-all-start.1) | async-done | bytes 1835040 | tf_op jit(solution)/shard_map/all_to_all | solution.py:92
  600.6 2.4 copy.40
  603.0 15.2 %convolution_convert_fusion = bf16[4096,896]{1,0:T(8,128)(2,1)} fusion(bf16[1024,4096]{1,0:T(8,128)(2,1)} %all-gather.14.cloned.1.call-done, bf16[1024,896]{1,0:T(8,128)(2,1)} %bitcast.38), kind=kOutput, calls=%fused_computation | convolution fusion | flops 7519862784 | bytes 17563648 | tf_op jit(solution)/shard_map/dot_general | solution.py:101
  618.1 33.3 %all-gather.12.cloned.1.call-done = bf16[1024,4096]{1,0:T(8,128)(2,1)} async-done(((bf16[256,4096]{1,0:T(8,128)(2,1)}), bf16[1024,4096]{1,0:T(8,128)(2,1)}) %all-gather.12.cloned.1.call-update) | async-done | bytes 8388624 | tf_op jit(solution)/shard_map/all_gather | solution.py:96
  651.4 12.1 %convolution_convert_fusion.1 = bf16[896,4096]{1,0:T(8,128)(2,1)} fusion(bf16[1024,896]{1,0:T(8,128)(2,1)S(1)} %bitcast.37, bf16[1024,4096]{1,0:T(8,128)(2,1)} %all-gather.12.cloned.1.call-done), kind=kOutput, calls=%fused_computation.1 | convolution fusion | flops 7519862784 | bytes 17563648 | tf_op jit(solution)/shard_map/dot_general | solution.py:98
  (31 shorter events, 0.1 us)
Async XLA Ops:
  7.2 52.6 %all-gather.6.cloned.1.call-start = ((), (), s32[]{:S(2)}) async-start(), calls=%async_computation.4 | async-start | bytes 2064384 | tf_op jit(solution)/shard_map/all_gather | solution.py:34
  9.8 175.5 %all-reduce.2.cloned.1.call-start = ((), (), s32[]{:S(2)}) async-start(), calls=%async_computation.5 | async-start | bytes 3670016 | tf_op jit(solution)/shard_map/psum | solution.py:40
  75.0 15.5 %copy-start = (bf16[256,4096]{1,0:T(8,128)(2,1)}, bf16[256,4096]{1,0:T(8,128)(2,1)S(1)}, u32[]{:S(2)}) copy-start(bf16[256,4096]{1,0:T(8,128)(2,1)S(1)} %get-tuple-element.4) | copy-start | bytes 6291460
  75.0 15.8 %copy-start.5 = (bf16[3584]{0:T(1024)(128)(2,1)S(1)}, bf16[3584]{0:T(1024)(128)(2,1)}, u32[]{:S(2)}) copy-start(bf16[3584]{0:T(1024)(128)(2,1)} %param.16) | copy-start | bytes 21508
  75.0 15.8 %copy-start.6 = (bf16[3584]{0:T(1024)(128)(2,1)S(1)}, bf16[3584]{0:T(1024)(128)(2,1)}, u32[]{:S(2)}) copy-start(bf16[3584]{0:T(1024)(128)(2,1)} %param.17) | copy-start | bytes 21508
  90.5 177.2 %reduce-scatter.7.cloned.1.call-start = ((), (), s32[]{:S(2)}) async-start(), calls=%async_computation.10 | async-start | bytes 2064384
  185.2 9.6 %slice-start = ((s8[6422528]{0:T(1024)(128)(4,1)}), s8[4194304]{0:T(1024)(128)(4,1)S(1)}, s32[]{:S(2)}) async-start(s8[6422528]{0:T(1024)(128)(4,1)} %bitcast.29), calls=%async_computation.12 | async-start | bytes 8388608
  189.2 5.7 slice-start.1
  189.2 5.7 copy-start.3
  189.2 7.9 %slice-start.4 = ((s8[6422528]{0:T(1024)(128)(4,1)}), s8[4194304]{0:T(1024)(128)(4,1)S(1)}, s32[]{:S(2)}) async-start(s8[6422528]{0:T(1024)(128)(4,1)} %bitcast.41), calls=%async_computation.16 | async-start | bytes 8388608
  194.9 2.2 slice-start.5
  197.1 4.4 copy-start.4
  201.4 154.0 %all-gather.8.cloned.1.call-start = ((), (), s32[]{:S(2)}) async-start(), calls=%async_computation.6 | async-start | bytes 2064384 | tf_op jit(solution)/shard_map/all_gather | solution.py:66
  309.2 126.3 %reduce-scatter.9.cloned.1.call-start = ((), (), s32[]{:S(2)}) async-start(), calls=%async_computation.11 | async-start | bytes 2064384
  355.3 11.1 %slice-start.2 = ((s8[6422528]{0:T(1024)(128)(4,1)}), s8[2228224]{0:T(1024)(128)(4,1)S(1)}, s32[]{:S(2)}) async-start(s8[6422528]{0:T(1024)(128)(4,1)} %bitcast.31), calls=%async_computation.14 | async-start | bytes 4456448
  361.0 5.5 slice-start.3
  370.1 134.3 %all-gather.10.cloned.1.call-start = ((), (), s32[]{:S(2)}) async-start(), calls=%async_computation.7 | async-start | bytes 2064384 | tf_op jit(solution)/shard_map/all_gather | solution.py:85
  459.7 143.3 %all-gather.14.cloned.1.call-start = ((), (), s32[]{:S(2)}) async-start(), calls=%async_computation.9 | async-start | bytes 10485760 | tf_op jit(solution)/shard_map/all_gather | solution.py:95
  460.4 191.0 %all-gather.12.cloned.1.call-start = ((), (), s32[]{:S(2)}) async-start(), calls=%async_computation.8 | async-start | bytes 10485760 | tf_op jit(solution)/shard_map/all_gather | solution.py:96
  504.5 18.4 %copy-start.1 = (bf16[256,3584]{0,1:T(8,128)(2,1)S(1)}, bf16[256,3584]{0,1:T(8,128)(2,1)}, u32[]{:S(2)}) copy-start(bf16[256,3584]{0,1:T(8,128)(2,1)} %all-gather.6.cloned.1.call-done) | copy-start | bytes 5505028
  569.0 31.6 %all-to-all-start.1 = ((bf16[256,4,896]{0,2,1:T(8,128)(2,1)}), bf16[256,4,896]{0,2,1:T(8,128)(2,1)S(1)}, u32[]{:S(2)}, u32[]{:S(2)}) async-start(bf16[256,4,896]{0,2,1:T(8,128)(2,1)} %bitcast.36), calls=%async_computation.1 | async-start | bytes 3670016 | tf_op jit(solution)/shard_map/all_to_all | solution.py:92
  603.0 48.5 %copy-start.2 = (bf16[4,256,896]{2,1,0:T(8,128)(2,1)S(1)}, bf16[4,256,896]{2,1,0:T(8,128)(2,1)}, u32[]{:S(2)}) copy-start(bf16[4,256,896]{2,1,0:T(8,128)(2,1)} %copy.34) | copy-start | bytes 5505028
Sparse Core Ops, SparseCore 0:
  10.6 49.1 all-gather.5
  90.6 94.5 all-reduce.1
  201.5 66.1 reduce-scatter.6
  309.4 45.9 all-gather.7
  370.3 65.1 reduce-scatter.8
  459.8 44.6 all-gather.9
  506.0 81.8 all-gather.13
  590.1 61.2 all-gather.11
where the time goes:
time: 671 us; the launch traced here: 670 us
  waiting for transfers between devices  422 us (63%)
  matrix products  103 us (15%)
  blocking collectives  102 us (15%)
  between operations  14.4 us (2%)
  other arithmetic  13.9 us (2%)
  local copies, waits for them, and re-layouts  10.9 us (2%)
    unnamed x10, waiting for transfers between devices  131 us
    psum x1, waiting for transfers between devices, per_device(): lax.psum(partial_recon.astype(jnp.bfloat16), ('tensor', 'latent'))  94.5 us
    all_gather x1, waiting for transfers between devices, per_device(): lax.all_gather(centered_share, ('tensor', 'latent'), axis=1, tiled=True)  49.3 us
    all_to_all x1, blocking collectives, per_device(): lax.all_to_all(centered, 'batch', split_axis=1, concat_axis=0, tiled=True)  46.2 us
    all_gather x1, waiting for transfers between devices, per_device(): lax.all_gather(grad_share, ('tensor', 'latent'), axis=1, tiled=True)  45.8 us
    all_gather x1, waiting for transfers between devices, per_device(): lax.all_gather(recon_share, ('tensor', 'latent'), axis=1, tiled=True)  44 us
    all_gather x1, waiting for transfers between devices, per_device(): lax.all_gather(grad_preact, 'batch', axis=0, tiled=True)  33.3 us
    all_to_all x1, waiting for transfers between devices, per_device(): lax.all_to_all(grad_recon, 'batch', split_axis=1, concat_axis=0, tiled=True)  24.1 us
  transfers between devices with their start and end apart: 9, of which 8 were waited for; matrix products, arithmetic and copies ran while one was open for 6% of the time, Pallas kernels for 0%

commit v1 on v0

v1 whole, which is shorter than its diff:
```python
import functools

import jax
import jax.numpy as jnp
from jax import lax
from jax.experimental import pallas as pl
from jax.experimental.pallas import tpu as pltpu
from jax.sharding import PartitionSpec as P

epsilon = 1e-06
MESH = pl.DeviceIdType.MESH
f32 = jnp.float32
bf16 = jnp.bfloat16


def far_first(n):
    return sorted(range(1, n), key=lambda e: -min(e, n - e))


def remote(src, dst, send, recv, **where):
    return pltpu.make_async_remote_copy(
        src_ref=src, dst_ref=dst, send_sem=send, recv_sem=recv, device_id=where, device_id_type=MESH
    )


def place(nt, nz):
    t, z = lax.axis_index("tensor"), lax.axis_index("latent")
    return t, z, lambda d: lax.rem(t + d, nt), lambda e: lax.rem(z + e, nz)


def meet(peers):
    barrier = pltpu.get_barrier_semaphore()
    for where in peers:
        pl.semaphore_signal(barrier, inc=1, device_id=where, device_id_type=MESH)
    pl.semaphore_wait(barrier, len(peers))


def gather_copies(nt, nz, part, lat_send, lat_recv, ten_send, ten_recv):
    t, z, tt, zz = place(nt, nz)
    sends = []
    own = part(t, z)
    for e in far_first(nz):
        c = remote(own, own, lat_send.at[e], lat_recv.at[e], latent=zz(e))
        c.start()
        sends.append(c)
    for d in range(1, nt):
        c = remote(own, own, ten_send.at[d, 0], ten_recv.at[d, 0], tensor=tt(d))
        c.start()
        sends.append(c)
    for e in reversed(far_first(nz)):
        came = part(t, zz(nz - e))
        remote(came, came, lat_send.at[e], lat_recv.at[e], latent=zz(e)).wait_recv()
        for d in range(1, nt):
            c = remote(came, came, ten_send.at[d, e], ten_recv.at[d, e], tensor=tt(d))
            c.start()
            sends.append(c)
    for d in range(1, nt):
        for e in range(nz):
            came = part(tt(nt - d), zz(nz - e))
            remote(came, came, ten_send.at[d, e], ten_recv.at[d, e], tensor=tt(d)).wait_recv()
    for c in sends:
        c.wait_send()


def first_kernel(
    nt, nz, centered_ref, target_ref, out_ref, rows_ref,
    lat_send, lat_recv, ten_send, ten_recv, row_send, row_recv,
):
    t, z, tt, zz = place(nt, nz)
    rows = target_ref.shape[0] // (nt * nz)
    others = [(d, e) for d in range(nt) for e in range(nz) if d or e]
    me = t * nz + z
    out_ref[me] = centered_ref[...]
    mine = pl.ds(pl.multiple_of(me * rows, rows), rows)
    rows_ref[me] = target_ref[mine]
    meet([{"tensor": tt(d), "latent": zz(e)} for d, e in others])
    copies = []
    for d, e in others:
        there = pl.ds(pl.multiple_of((tt(d) * nz + zz(e)) * rows, rows), rows)
        c = remote(
            target_ref.at[there], rows_ref.at[me], row_send.at[d, e], row_recv.at[d, e],
            tensor=tt(d), latent=zz(e),
        )
        c.start()
        copies.append(c)
    gather_copies(
        nt, nz, lambda a, b: out_ref.at[a * nz + b], lat_send, lat_recv, ten_send, ten_recv
    )
    for (d, e), c in zip(others, copies):
        c.wait_send()
        slot = rows_ref.at[tt(nt - d) * nz + zz(nz - e)]
        remote(
            slot, slot, row_send.at[d, e], row_recv.at[d, e], tensor=tt(d), latent=zz(e)
        ).wait_recv()


def exchange_kernel(nt, nz, inputs, outputs, row_math, partial_ref, *refs):
    ins = refs[:inputs]
    out_ref = refs[inputs]
    outs = refs[inputs + 1 : inputs + 1 + outputs]
    (
        ten_buf, sum_buf, lat_buf, xs, xr, ys, yr, lat_send, lat_recv, ten_send, ten_recv,
    ) = refs[inputs + 1 + outputs :]
    t, z, tt, zz = place(nt, nz)
    rows = partial_ref.shape[0] // (nt * nz)

    def part_rows(a, b):
        return pl.ds(pl.multiple_of((a * nz + b) * rows, rows), rows)

    meet(
        [{"tensor": tt(d)} for d in range(1, nt)] + [{"latent": zz(e)} for e in range(1, nz)]
    )
    order = far_first(nz) + [0]
    sends = []
    firsts = {}
    for e in order:
        for d in range(1, nt):
            c = remote(
                partial_ref.at[part_rows(tt(d), zz(e))], ten_buf.at[d - 1, e],
                xs.at[d, e], xr.at[d, e], tensor=tt(d),
            )
            c.start()
            firsts[d, e] = c
    total = None
    for e in order:
        total = partial_ref[part_rows(t, zz(e))].astype(f32)
        for d in range(1, nt):
            firsts[d, e].wait()
            total = total + ten_buf[d - 1, e].astype(f32)
        if e:
            sum_buf[e - 1] = total.astype(bf16)
            c = remote(
                sum_buf.at[e - 1], lat_buf.at[e - 1], ys.at[e], yr.at[e], latent=zz(e)
            )
            c.start()
            sends.append(c)
    for c in sends:
        c.wait()
    for e in range(1, nz):
        total = total + lat_buf[e - 1].astype(f32)
    row_math(total, ins, outs, lambda value: out_ref.__setitem__(part_rows(t, z), value))
    gather_copies(
        nt, nz, lambda a, b: out_ref.at[part_rows(a, b)], lat_send, lat_recv, ten_send, ten_recv
    )


def mean_square_scale(rows):
    return lax.rsqrt(jnp.mean(rows * rows, axis=1, keepdims=True) + epsilon)


def recon_math(total, ins, outs, put):
    bias, gain = ins
    recon = total + bias[...].astype(f32)
    outs[0][...] = recon
    put((recon * mean_square_scale(recon) * gain[...].astype(f32)).astype(bf16))


def output_math(token_count, total, ins, outs, put):
    recon, target, gain_ref = ins
    gain = gain_ref[...].astype(f32)
    scale_out = mean_square_scale(total)
    normed_out = total * scale_out
    result = recon[...] + normed_out * gain
    grad_result = (2.0 / token_count) * (result - target[...].astype(f32))
    outs[0][...] = grad_result
    grad_normed = grad_result * gain
    inner = jnp.mean(grad_normed * normed_out, axis=1, keepdims=True)
    put((scale_out * (grad_normed - normed_out * inner)).astype(bf16))


def input_math(total, ins, outs, put):
    recon_ref, grad_result, gain = ins
    recon = recon_ref[...]
    scale_in = mean_square_scale(recon)
    unit = recon * scale_in
    grad_unit = total * gain[...].astype(f32)
    inner = jnp.mean(grad_unit * unit, axis=1, keepdims=True)
    put((grad_result[...] + scale_in * (grad_unit - unit * inner)).astype(bf16))


VMEM = pl.BlockSpec(memory_space=pltpu.VMEM)
DMA = pltpu.SemaphoreType.DMA


def priced(byte_count):
    return pl.CostEstimate(flops=0, bytes_accessed=byte_count, transcendentals=0)


def exchange(nt, nz, ident, row_math, partial, ins, row_outputs):
    tokens, width = partial.shape
    rows = tokens // (nt * nz)
    shape = jax.ShapeDtypeStruct
    return pl.pallas_call(
        functools.partial(exchange_kernel, nt, nz, len(ins), row_outputs, row_math),
        out_shape=[shape((tokens, width), bf16)] + [shape((rows, width), f32)] * row_outputs,
        in_specs=[VMEM] * (1 + len(ins)),
        out_specs=[VMEM] * (1 + row_outputs),
        scratch_shapes=[
            pltpu.VMEM((max(nt - 1, 1), nz, rows, width), bf16),
            pltpu.VMEM((max(nz - 1, 1), rows, width), bf16),
            pltpu.VMEM((max(nz - 1, 1), rows, width), bf16),
            DMA((nt, nz)), DMA((nt, nz)), DMA((nz,)), DMA((nz,)),
            DMA((nz,)), DMA((nz,)), DMA((nt, nz)), DMA((nt, nz)),
        ],
        compiler_params=pltpu.CompilerParams(collective_id=ident, has_side_effects=True),
        cost_estimate=priced(100_000_000),
        name=f"exchange_{ident}",
    )(partial, *ins)


def swap(x, k):
    n = lax.axis_size("batch")
    return lax.ppermute(x, "batch", [(i, i ^ k) for i in range(n)])


def spread(x):
    pieces = [x]
    for k in range(1, lax.axis_size("batch")):
        pieces.append(swap(pieces[k - 1], 1) if k > 1 and k % 2 else swap(x, k))
    return pieces


def blocks(x):
    n = lax.axis_size("batch")
    b = lax.axis_index("batch")
    width = x.shape[1] // n
    return [
        swap(part, k) if k else part
        for k in range(n)
        for part in [lax.dynamic_slice_in_dim(x, (b ^ k) * width, width, 1)]
    ]


def per_device(
    residual, target, encoder_weight, encoder_bias, decoder_weight, decoder_bias,
    first_gain, second_gain, gate_weight, up_weight, down_weight,
):
    contract_last = (((1,), (1,)), ((), ()))
    contract_first = (((0,), (0,)), ((), ()))
    nt, nz = lax.axis_size("tensor"), lax.axis_size("latent")
    n = nt * nz
    tokens, share = residual.shape
    width = share * n
    rows = tokens // n
    token_count = tokens * lax.axis_size("batch")
    offset = lax.axis_index(("tensor", "latent")) * share
    bias_share = lax.dynamic_slice_in_dim(decoder_bias.astype(f32), offset, share)
    centered_share = (residual.astype(f32) - bias_share).astype(bf16)
    shape = jax.ShapeDtypeStruct
    gathered, target_parts = pl.pallas_call(
        functools.partial(first_kernel, nt, nz),
        out_shape=[shape((n, tokens, share), bf16), shape((n, rows, share), bf16)],
        in_specs=[VMEM] * 2,
        out_specs=[VMEM] * 2,
        scratch_shapes=[
            DMA((nz,)), DMA((nz,)), DMA((nt, nz)), DMA((nt, nz)), DMA((nt, nz)), DMA((nt, nz)),
        ],
        compiler_params=pltpu.CompilerParams(collective_id=0, has_side_effects=True),
        cost_estimate=priced(60_000_000),
        name="exchange_0",
    )(centered_share, target)
    centered = gathered.transpose(1, 0, 2).reshape(tokens, width)
    target_rows = target_parts.transpose(1, 0, 2).reshape(rows, width)

    preact = jnp.dot(centered, encoder_weight, preferred_element_type=f32)
    latents = jnp.maximum(preact + encoder_bias.astype(f32), 0.0).astype(bf16)
    latent_pieces = spread(latents)
    centered_pieces = blocks(centered)
    partial_recon = jnp.dot(latents, decoder_weight, preferred_element_type=f32).astype(bf16)
    bias, gain_in, gain_out = (v.reshape(1, width) for v in (decoder_bias, first_gain, second_gain))
    normed_input, recon = exchange(nt, nz, 1, recon_math, partial_recon, (bias, gain_in), 1)
    gate_value = jnp.dot(normed_input, gate_weight, preferred_element_type=f32)
    up_value = jnp.dot(normed_input, up_weight, preferred_element_type=f32)
    gelu_value, gelu_back = jax.vjp(lambda v: jax.nn.gelu(v, approximate=True), gate_value)
    hidden = (gelu_value * up_value).astype(bf16)
    partial_out = jnp.dot(hidden, down_weight, preferred_element_type=f32).astype(bf16)
    grad_output, grad_result = exchange(
        nt, nz, 2, functools.partial(output_math, token_count), partial_out,
        (recon, target_rows, gain_out), 1,
    )
    grad_hidden = lax.dot_general(
        grad_output, down_weight, contract_last, preferred_element_type=f32
    )
    grad_gate = gelu_back(grad_hidden * up_value)[0].astype(bf16)
    grad_up = (grad_hidden * gelu_value).astype(bf16)
    partial_input = lax.dot_general(
        grad_gate, gate_weight, contract_last, preferred_element_type=f32
    )
    partial_input = partial_input + lax.dot_general(
        grad_up, up_weight, contract_last, preferred_element_type=f32
    )
    partial_input, latent_pieces, centered_pieces = lax.optimization_barrier(
        (partial_input.astype(bf16), latent_pieces, centered_pieces)
    )
    latents_all = jnp.concatenate(latent_pieces, axis=0)
    centered_block = jnp.concatenate(centered_pieces, axis=0)
    (grad_recon,) = exchange(
        nt, nz, 3, input_math, partial_input, (recon, grad_result, gain_in), 0
    )
    chunks = 4
    step = latents.shape[1] // chunks
    spread_chunks = []
    for c in range(chunks):
        grad_latent = lax.dot_general(
            grad_recon, decoder_weight[c * step : (c + 1) * step], contract_last,
            preferred_element_type=f32,
        )
        mask = latents[:, c * step : (c + 1) * step] > 0
        spread_chunks.append(spread(jnp.where(mask, grad_latent, 0.0).astype(bf16)))
    recon_block = jnp.concatenate(blocks(grad_recon), axis=0)
    decoder_grad = lax.dot_general(
        latents_all, recon_block, contract_first, preferred_element_type=f32
    ).astype(bf16)
    encoder_grad = jnp.concatenate(
        [
            lax.dot_general(
                centered_block, jnp.concatenate(pieces, axis=0), contract_first,
                preferred_element_type=f32,
            ).astype(bf16)
            for pieces in spread_chunks
        ],
        axis=1,
    )
    return (encoder_grad, decoder_grad)


def solution(mesh):
    in_specs = (
        P("batch", ("tensor", "latent")),
        P("batch", ("tensor", "latent")),
        P(None, ("tensor", "latent")),
        P(("tensor", "latent")),
        P(("tensor", "latent"), None),
        P(),
        P(),
        P(),
        P(None, ("tensor", "latent")),
        P(None, ("tensor", "latent")),
        P(("tensor", "latent"), None),
    )
    out_specs = (P("batch", ("tensor", "latent")), P(("tensor", "latent"), "batch"))
    return jax.shard_map(
        per_device, mesh=mesh, in_specs=in_specs, out_specs=out_specs, check_vma=False
    )
```

time: 671 us -> 442 us (0.66)
  waiting for transfers between devices: 422 us -> 38.7 us
  Pallas kernels: 0 us -> 262 us
  blocking collectives: 102 us -> 0 us
  between operations: 14.4 us -> 1.61 us
  starting transfers between devices: 4.57 us -> 14.3 us
  other arithmetic: 13.9 us -> 5.59 us
    pallas_call x0 -> x4, Pallas kernels: none -> 262 us  [the longest x3 223 us: exchange(): pl.pallas_call(functools.partial(exchange_kernel, nt, nz, len(ins), row_o...]
    all_gather x5 -> x0, waiting for transfers between devices: 172 us -> none  [the longest x1 49.3 us: per_device(): lax.all_gather(centered_share, ('tensor', 'latent'), axis=1, tiled=True)]
    unnamed x10 -> x0, waiting for transfers between devices: 131 us -> none
    psum x1 -> x0, waiting for transfers between devices: 94.5 us -> none  [per_device(): lax.psum(partial_recon.astype(jnp.bfloat16), ('tensor', 'latent'))]
    psum x3 -> x0, blocking collectives: 55.9 us -> none  [the longest x1 19.4 us: per_device(): lax.psum(jnp.sum(output * output, axis=1), ('tensor', 'latent'))]
    all_to_all x1 -> x0, blocking collectives: 46.2 us -> none  [per_device(): lax.all_to_all(centered, 'batch', split_axis=1, concat_axis=0, tiled=True)]
    ppermute x0 -> x21, waiting for transfers between devices: none -> 38.7 us  [swap(): return lax.ppermute(x, 'batch', [(i, i ^ k) for i in range(n)])]
    all_to_all x1 -> x0, waiting for transfers between devices: 24.1 us -> none  [per_device(): lax.all_to_all(grad_recon, 'batch', split_axis=1, concat_axis=0, tiled=True)]
  transfers between devices with their start and end apart: 9 -> 21, of which waited for: 8 -> 4; matrix products, arithmetic and copies ran while one was open for 6% -> 17% of each run, Pallas kernels for 0% -> 34%
where the time goes in v1:
time: 442 us; the launch traced here: 435 us
  Pallas kernels  262 us (59%)
  matrix products  99.2 us (22%)
  waiting for transfers between devices  38.7 us (9%)
  starting transfers between devices  14.3 us (3%)
  local copies, waits for them, and re-layouts  13.9 us (3%)
  other arithmetic  5.59 us (1%)
    pallas_call x3, Pallas kernels, exchange(): pl.pallas_call(functools.partial(exchange_kernel, nt, nz, len(ins), row_o...  223 us
    pallas_call x1, Pallas kernels, per_device(): pl.pallas_call(functools.partial(first_kernel, nt, nz), out_shape=[shape(...  39.1 us
    ppermute x21, waiting for transfers between devices, swap(): return lax.ppermute(x, 'batch', [(i, i ^ k) for i in range(n)])  38.7 us
    dot_general x4, matrix products, per_device(): lax.dot_general(grad_recon, decoder_weight[c * step:(c + 1) * step], cont...  21.7 us
    dot_general x1, matrix products, per_device(): preact = jnp.dot(centered, encoder_weight, preferred_element_type=f32)  15.1 us
    dot_general x1, matrix products, per_device(): jnp.dot(latents, decoder_weight, preferred_element_type=f32).astype(bf16)  15 us
    ppermute x21, starting transfers between devices, swap(): return lax.ppermute(x, 'batch', [(i, i ^ k) for i in range(n)])  14.3 us
    dot_general x1, matrix products, per_device(): lax.dot_general(latents_all, recon_block, contract_first, preferred_eleme...  13.6 us
  transfers between devices with their start and end apart: 21, of which 4 were waited for; matrix products, arithmetic and copies ran while one was open for 17% of the time, Pallas kernels for 34%

profile of v1, /device:TPU:0, one launch (start us, length us, event | category | flops | bytes accessed | tf_op | source)
XLA Modules:
  0.0 435.1 jit_solution(10233021694420478105)
XLA Ops:
  0.6 0.7 convert_element_type.63
  1.3 1.8 copy.21.target_ref
  3.1 1.1 copy.20
  4.2 0.8 dynamic-slice_convert_fusion
  5.0 0.7 subtract_convert_fusion.centered_ref
  5.7 39.1 %exchange_0.1 = (bf16[8,256,448]{2,1,0:T(8,128)(2,1)}, bf16[8,32,448]{2,1,0:T(8,128)(2,1)}) custom-call(bf16[256,448]{1,0:T(8,128)(2,1)} %subtract_convert_fusion.centered_ref, bf16[256,448]{1,0:T(8,128)(2,1)} %copy.21.target_ref), custom_call_target="tpu_custom_call" | custom-call | bytes 60000000 | tf_op jit(solution)/shard_map/exchange_0/pallas_call | solution.py:250
  44.8 3.3 copy.22
  48.1 15.1 %fusion.20 = bf16[256,4096]{1,0:T(8,128)(2,1)} fusion(bf16[256,3584]{0,1:T(8,128)(2,1)S(1)} %bitcast.24, bf16[3584,4096]{1,0:T(8,128)(2,1)} %param.13, f32[4096]{0:T(1024)S(1)} %convert_element_type.63), kind=kOutput, calls=%fused_computation.21 | convolution fusion | flops 7519338496 | bytes 33308672 | tf_op jit(solution)/shard_map/dot_general | solution.py:265
  63.2 1.5 collective-permute-start.1
  64.7 1.1 constant_dynamic-slice_fusion.4
  65.8 0.6 collective-permute-start.5
  66.4 1.5 collective-permute-start.4
  67.9 15.0 %convolution_convert_fusion.partial_ref = bf16[256,3584]{1,0:T(8,128)(2,1)} fusion(bf16[256,4096]{1,0:T(8,128)(2,1)} %fusion.20, bf16[4096,3584]{1,0:T(8,128)(2,1)} %param.15), kind=kOutput, calls=%fused_computation.22 | convolution fusion | flops 7517110272 | bytes 33292288 | tf_op jit(solution)/shard_map/dot_general | solution.py:269
  82.9 0.6 reshape.22.refs_0_
  83.5 0.6 reshape.23.refs_1_.refs_2_
  84.2 75.8 %exchange_1.1 = (bf16[256,3584]{1,0:T(8,128)(2,1)}, f32[32,3584]{1,0:T(8,128)}) custom-call(bf16[256,3584]{1,0:T(8,128)(2,1)} %convolution_convert_fusion.partial_ref, bf16[1,3584]{1,0:T(2,128)(2,1)} %reshape.22.refs_0_, bf16[1,3584]{1,0:T(2,128)(2,1)} %reshape.23.refs_1_.refs_2_), custom_call_target="tpu_custom_call" | custom-call | bytes 100000000 | tf_op jit(solution)/shard_map/exchange_1/pallas_call | solution.py:193
  160.0 0.0 slice-start.1
  160.0 0.0 slice-start.4
  160.0 5.6 %fusion.131 = f32[256,896]{1,0:T(8,128)S(1)} fusion(bf16[256,3584]{1,0:T(8,128)(2,1)} %get-tuple-element.18, bf16[3584,896]{1,0:T(8,128)(2,1)} %param.19), kind=kOutput, calls=%fused_computation.128 | convolution fusion | flops 1644167168 | bytes 9175040 | tf_op jit(solution)/shard_map/dot_general | solution.py:272
  165.6 0.0 slice-start.5
  165.7 2.1 fusion.132
  167.8 0.1 collective-permute-start.2
  167.9 3.5 convolution_convert_fusion.1.partial_ref
  171.4 0.6 reshape.25.refs_2_
  172.0 0.1 copy.23
  172.1 1.0 reshape.24.refs_1_
  173.1 71.7 %exchange_2.1 = (bf16[256,3584]{1,0:T(8,128)(2,1)}, f32[32,3584]{1,0:T(8,128)}) custom-call(bf16[256,3584]{1,0:T(8,128)(2,1)} %convolution_convert_fusion.1.partial_ref, f32[32,3584]{1,0:T(8,128)} %get-tuple-element.19.refs_0_, bf16[32,3584]{1,0:T(8,128)(2,1)} %reshape.24.refs_1_, bf16[1,3584]{1,0:T(2,128)(2,1)} %reshape.25.refs_2_), custom_call_target="tpu_custom_call" | custom-call | bytes 100000000 | tf_op jit(solution)/shard_map/exchange_2/pallas_call | solution.py:193
  244.8 5.6 %fusion.133 = f32[256,896]{1,0:T(8,128)S(1)} fusion(bf16[256,3584]{1,0:T(8,128)(2,1)} %get-tuple-element.21, bf16[896,3584]{1,0:T(8,128)(2,1)} %param.21), kind=kOutput, calls=%fused_computation.130 | convolution fusion | flops 1644167168 | bytes 9175040 | tf_op jit(solution)/shard_map/dot_general | solution.py:281
  250.4 0.0 slice-start.3
  250.5 5.4 %fusion.104 = f32[256,3584]{1,0:T(8,128)S(1)} fusion(bf16[3584,896]{1,0:T(8,128)(2,1)} %param.19, f32[256,896]{1,0:T(8,128)S(1)} %copy-done.2, f32[256,896]{1,0:T(8,128)S(1)} %fusion.133, f32[256,896]{1,0:T(8,128)S(1)} %copy-done.10), kind=kOutput, calls=%fused_computation.89 | convolution fusion | flops 1648984064 | bytes 12845056 | tf_op jit(solution)/shard_map/dot_general | solution.py:286
  255.9 3.4 fusion.21.partial_ref
  259.4 75.2 %exchange_3.1 = bf16[256,3584]{1,0:T(8,128)(2,1)} custom-call(bf16[256,3584]{1,0:T(8,128)(2,1)} %fusion.21.partial_ref, f32[32,3584]{1,0:T(8,128)} %get-tuple-element.19.refs_0_, f32[32,3584]{1,0:T(8,128)} %get-tuple-element.27.refs_1_, bf16[1,3584]{1,0:T(2,128)(2,1)} %reshape.23.refs_1_.refs_2_), custom_call_target="tpu_custom_call" | custom-call | bytes 100000000 | tf_op jit(solution)/shard_map/exchange_3/pallas_call | solution.py:193
  334.5 5.9 %fusion.94 = bf16[256,1024]{1,0:T(8,128)(2,1)S(1)} fusion(bf16[256,3584]{1,0:T(8,128)(2,1)} %exchange_3.1, bf16[4096,3584]{1,0:T(8,128)(2,1)} %param.15, bf16[256,4096]{1,0:T(8,128)(2,1)} %fusion.20), kind=kOutput, calls=%fused_computation.77 | convolution fusion | flops 1879834624 | bytes 10223616 | tf_op jit(solution)/shard_map/dot_general | solution.py:304
  340.4 5.2 %fusion.88 = bf16[256,1024]{1,0:T(8,128)(2,1)S(1)} fusion(bf16[256,3584]{1,0:T(8,128)(2,1)S(1)} %copy-done, bf16[4096,3584]{1,0:T(8,128)(2,1)} %param.15, bf16[256,4096]{1,0:T(8,128)(2,1)} %fusion.20), kind=kOutput, calls=%fused_computation.75 | convolution fusion | flops 1879834624 | bytes 10223616 | tf_op jit(solution)/shard_map/dot_general | solution.py:304
  345.7 5.2 %fusion.76 = bf16[256,1024]{1,0:T(8,128)(2,1)S(1)} fusion(bf16[256,3584]{1,0:T(8,128)(2,1)S(1)} %copy-done, bf16[4096,3584]{1,0:T(8,128)(2,1)} %param.15, bf16[256,4096]{1,0:T(8,128)(2,1)} %fusion.20), kind=kOutput, calls=%fused_computation.71 | convolution fusion | flops 1879834624 | bytes 10223616 | tf_op jit(solution)/shard_map/dot_general | solution.py:304
  350.9 0.2 constant_dynamic-slice_fusion.3
  351.1 0.1 collective-permute-start.20
  351.2 0.6 collective-permute-start.19
  351.7 1.3 collective-permute-start.18
  353.0 0.5 collective-permute-start.7
  353.5 1.5 collective-permute-start.16
  355.1 1.1 constant_dynamic-update-slice_fusion.2
  356.2 1.1 constant_dynamic-update-slice_fusion.1
  357.3 1.1 constant_dynamic-update-slice_fusion
  358.4 5.4 %fusion.82 = bf16[256,1024]{1,0:T(8,128)(2,1)S(1)} fusion(bf16[256,3584]{1,0:T(8,128)(2,1)S(1)} %copy-done, bf16[4096,3584]{1,0:T(8,128)(2,1)} %param.15, bf16[256,4096]{1,0:T(8,128)(2,1)} %fusion.20), kind=kOutput, calls=%fused_computation.73 | convolution fusion | flops 1879834624 | bytes 10223616 | tf_op jit(solution)/shard_map/dot_general | solution.py:304
  363.7 0.3 collective-permute-done.20
  364.0 7.9 %collective-permute-done.19 = bf16[256,896]{1,0:T(8,128)(2,1)S(1)} collective-permute-done((bf16[256,896]{1,0:T(8,128)(2,1)S(1)}, bf16[256,896]{1,0:T(8,128)(2,1)S(1)}, u32[]{:S(2)}, u32[]{:S(2)}) %collective-permute-start.19) | collective-permute-done | bytes 458784 | tf_op jit(solution)/shard_map/ppermute | solution.py:213
  371.9 2.0 collective-permute-start.15
  373.9 0.5 collective-permute-start.13
  374.5 0.2 copy-done.8
  374.7 19.7 %collective-permute-done.16 = bf16[256,1024]{1,0:T(8,128)(2,1)S(1)} collective-permute-done((bf16[256,1024]{1,0:T(8,128)(2,1)S(1)}, bf16[256,1024]{1,0:T(8,128)(2,1)S(1)}, u32[]{:S(2)}, u32[]{:S(2)}) %collective-permute-start.16) | collective-permute-done | bytes 524320 | tf_op jit(solution)/shard_map/ppermute | solution.py:213
  394.4 2.0 collective-permute-start.17
  396.4 13.6 %fusion.16 = bf16[4096,896]{1,0:T(8,128)(2,1)} fusion(bf16[256,4096]{1,0:T(8,128)(2,1)} %collective-permute-done.2, bf16[256,4096]{1,0:T(8,128)(2,1)} %collective-permute-done.1, bf16[256,4096]{1,0:T(8,128)(2,1)} %collective-permute-done, bf16[256,4096]{1,0:T(8,128)(2,1)} %fusion.20, bf16[256,896]{1,0:T(8,128)(2,1)S(1)} %collective-permute-done.20, ...), kind=kOutput, calls=%fused_computation.17 | convolution fusion | flops 7560757248 | bytes 17563648 | tf_op jit(solution)/shard_map/dot_general | solution.py:311
  410.0 0.1 collective-permute-start.12
  410.1 1.0 collective-permute-start.10
  411.1 2.1 fusion.61
  413.2 0.6 collective-permute-start.9
  413.7 10.7 %collective-permute-done.10 = bf16[256,1024]{1,0:T(8,128)(2,1)S(1)} collective-permute-done((bf16[256,1024]{1,0:T(8,128)(2,1)S(1)}, bf16[256,1024]{1,0:T(8,128)(2,1)S(1)}, u32[]{:S(2)}, u32[]{:S(2)}) %collective-permute-start.10) | collective-permute-done | bytes 524320 | tf_op jit(solution)/shard_map/ppermute | solution.py:213
  424.4 0.5 collective-permute-start.11
  425.0 2.1 fusion.64
  427.1 0.0 collective-permute-done.11
  427.1 2.1 fusion.67
  429.2 2.1 fusion.70
  431.3 3.4 pad_maximum_fusion
  (54 shorter events, 0.2 us)
Async XLA Ops:
  63.2 104.6 %collective-permute-start.1 = (bf16[256,4096]{1,0:T(8,128)(2,1)}, bf16[256,4096]{1,0:T(8,128)(2,1)}, u32[]{:S(2)}, u32[]{:S(2)}) collective-permute-start(bf16[256,4096]{1,0:T(8,128)(2,1)} %fusion.20), channel_id=1, source_target_pairs={{0,16},{8,24},{16,0},{24,8},{1,17},{9,25},{17,1},{25,9},{2,18},{10... | collective-permute-start | bytes 6291464 | tf_op jit(solution)/shard_map/ppermute | solution.py:213
  64.7 194.6 %collective-permute-start = (bf16[256,4096]{1,0:T(8,128)(2,1)}, bf16[256,4096]{1,0:T(8,128)(2,1)}, u32[]{:S(2)}, u32[]{:S(2)}) collective-permute-start(bf16[256,4096]{1,0:T(8,128)(2,1)} %fusion.20), channel_id=1, source_target_pairs={{0,8},{8,0},{16,24},{24,16},{1,9},{9,1},{17,25},{25,17},{2,10},{10... | collective-permute-start | bytes 6291464 | tf_op jit(solution)/shard_map/ppermute | solution.py:213
  65.8 193.5 %collective-permute-start.5 = (bf16[256,896]{0,1:T(8,128)(2,1)}, bf16[256,896]{0,1:T(8,128)(2,1)}, u32[]{:S(2)}, u32[]{:S(2)}) collective-permute-start(bf16[256,896]{0,1:T(8,128)(2,1)} %get-tuple-element.36), channel_id=1, source_target_pairs={{0,24},{8,16},{16,8},{24,0},{1,25},{9,17},{17,9},{25,1},{2,26},{10... | collective-permute-start | bytes 1376264 | tf_op jit(solution)/shard_map/ppermute | solution.py:213
  66.4 192.9 %collective-permute-start.4 = (bf16[256,896]{0,1:T(8,128)(2,1)}, bf16[256,896]{0,1:T(8,128)(2,1)}, u32[]{:S(2)}, u32[]{:S(2)}) collective-permute-start(bf16[256,896]{0,1:T(8,128)(2,1)} %get-tuple-element.37), channel_id=1, source_target_pairs={{0,16},{8,24},{16,0},{24,8},{1,17},{9,25},{17,1},{25,9},{2,18},{10... | collective-permute-start | bytes 1376264 | tf_op jit(solution)/shard_map/ppermute | solution.py:213
  67.9 15.0 %copy-start.4 = (bf16[3584]{0:T(1024)(128)(2,1)S(1)}, bf16[3584]{0:T(1024)(128)(2,1)}, u32[]{:S(2)}) copy-start(bf16[3584]{0:T(1024)(128)(2,1)} %param.16) | copy-start | bytes 21508
  67.9 15.6 %copy-start.5 = (bf16[3584]{0:T(1024)(128)(2,1)S(1)}, bf16[3584]{0:T(1024)(128)(2,1)}, u32[]{:S(2)}) copy-start(bf16[3584]{0:T(1024)(128)(2,1)} %param.17) | copy-start | bytes 21508
  67.9 191.4 %collective-permute-start.3 = (bf16[256,896]{0,1:T(8,128)(2,1)S(1)}, bf16[256,896]{0,1:T(8,128)(2,1)}, u32[]{:S(2)}, u32[]{:S(2)}) collective-permute-start(bf16[256,896]{0,1:T(8,128)(2,1)S(1)} %get-tuple-element.38), channel_id=1, source_target_pairs={{0,8},{8,0},{16,24},{24,16},{1,9},{9,1},{17,25},{25,17},{2,10},{10... | collective-permute-start | bytes 1376264 | tf_op jit(solution)/shard_map/ppermute | solution.py:213
  84.2 81.4 %slice-start = ((s8[6422528]{0:T(1024)(128)(4,1)}), s8[2228224]{0:T(1024)(128)(4,1)S(1)}, s32[]{:S(2)}) async-start(s8[6422528]{0:T(1024)(128)(4,1)} %bitcast.26), calls=%async_computation | async-start | bytes 4456448
  160.0 5.6 %slice-start.1 = ((s8[6422528]{0:T(1024)(128)(4,1)}), s8[4194304]{0:T(1024)(128)(4,1)S(1)}, s32[]{:S(2)}) async-start(s8[6422528]{0:T(1024)(128)(4,1)} %bitcast.26), calls=%async_computation.1 | async-start | bytes 8388608
  160.0 5.6 %copy-start.7 = (bf16[256,3584]{1,0:T(8,128)(2,1)S(1)}, bf16[256,3584]{1,0:T(8,128)(2,1)}, u32[]{:S(2)}) copy-start(bf16[256,3584]{1,0:T(8,128)(2,1)} %get-tuple-element.18) | copy-start | bytes 5505028
  160.0 7.9 %slice-start.4 = ((s8[6422528]{0:T(1024)(128)(4,1)}), s8[4194304]{0:T(1024)(128)(4,1)S(1)}, s32[]{:S(2)}) async-start(s8[6422528]{0:T(1024)(128)(4,1)} %bitcast.32), calls=%async_computation.4 | async-start | bytes 8388608
  165.6 2.2 copy-start.1
  165.6 2.2 slice-start.5
  167.7 3.6 copy-start.9
  167.7 3.6 copy-start.6
  167.7 4.2 copy-start.3
  167.8 91.6 %collective-permute-start.2 = (bf16[256,4096]{1,0:T(8,128)(2,1)}, bf16[256,4096]{1,0:T(8,128)(2,1)}, u32[]{:S(2)}, u32[]{:S(2)}) collective-permute-start(bf16[256,4096]{1,0:T(8,128)(2,1)} %collective-permute-done.1), channel_id=1, source_target_pairs={{0,8},{8,0},{16,24},{24,16},{1,9},{9,1},{17,25},{25,17},{2,10},{10... | collective-permute-start | bytes 6291464 | tf_op jit(solution)/shard_map/ppermute | solution.py:213
  244.8 5.6 %copy-start.2 = (f32[256,896]{1,0:T(8,128)S(1)}, f32[256,896]{1,0:T(8,128)}, u32[]{:S(2)}) copy-start(f32[256,896]{1,0:T(8,128)} %copy-done.1) | copy-start | bytes 2752516
  244.8 5.6 %copy-start.10 = (f32[256,896]{1,0:T(8,128)S(1)}, f32[256,896]{1,0:T(8,128)}, u32[]{:S(2)}) copy-start(f32[256,896]{1,0:T(8,128)} %copy-done.9) | copy-start | bytes 2752516
  244.8 11.1 %slice-start.2 = ((s8[6422528]{0:T(1024)(128)(4,1)}), s8[4194304]{0:T(1024)(128)(4,1)S(1)}, s32[]{:S(2)}) async-start(s8[6422528]{0:T(1024)(128)(4,1)} %bitcast.28), calls=%async_computation.2 | async-start | bytes 8388608
  250.4 5.5 %slice-start.3 = ((s8[6422528]{0:T(1024)(128)(4,1)}), s8[2228224]{0:T(1024)(128)(4,1)S(1)}, s32[]{:S(2)}) async-start(s8[6422528]{0:T(1024)(128)(4,1)} %bitcast.28), calls=%async_computation.3 | async-start | bytes 4456448
  334.5 5.9 %copy-start = (bf16[256,3584]{1,0:T(8,128)(2,1)S(1)}, bf16[256,3584]{1,0:T(8,128)(2,1)}, u32[]{:S(2)}) copy-start(bf16[256,3584]{1,0:T(8,128)(2,1)} %exchange_3.1) | copy-start | bytes 5505028
  351.1 12.9 %collective-permute-start.20 = (bf16[256,896]{1,0:T(8,128)(2,1)S(1)}, bf16[256,896]{1,0:T(8,128)(2,1)S(1)}, u32[]{:S(2)}, u32[]{:S(2)}) collective-permute-start(bf16[256,896]{1,0:T(8,128)(2,1)S(1)} %get-tuple-element.33), channel_id=1, source_target_pairs={{0,24},{8,16},{16,8},{24,0},{1,25},{9,17},{17,9},{25,1},{2,26},{10... | collective-permute-start | bytes 1376264 | tf_op jit(solution)/shard_map/ppermute | solution.py:213
  351.2 20.8 %collective-permute-start.19 = (bf16[256,896]{1,0:T(8,128)(2,1)S(1)}, bf16[256,896]{1,0:T(8,128)(2,1)S(1)}, u32[]{:S(2)}, u32[]{:S(2)}) collective-permute-start(bf16[256,896]{1,0:T(8,128)(2,1)S(1)} %get-tuple-element.34), channel_id=1, source_target_pairs={{0,16},{8,24},{16,0},{24,8},{1,17},{9,25},{17,1},{25,9},{2,18},{10... | collective-permute-start | bytes 1376264 | tf_op jit(solution)/shard_map/ppermute | solution.py:213
  351.7 22.2 %collective-permute-start.18 = (bf16[256,896]{1,0:T(8,128)(2,1)S(1)}, bf16[256,896]{1,0:T(8,128)(2,1)S(1)}, u32[]{:S(2)}, u32[]{:S(2)}) collective-permute-start(bf16[256,896]{1,0:T(8,128)(2,1)S(1)} %get-tuple-element.35), channel_id=1, source_target_pairs={{0,8},{8,0},{16,24},{24,16},{1,9},{9,1},{17,25},{25,17},{2,10},{10... | collective-permute-start | bytes 1376264 | tf_op jit(solution)/shard_map/ppermute | solution.py:213
  353.0 60.1 %collective-permute-start.7 = (bf16[256,1024]{1,0:T(8,128)(2,1)S(1)}, bf16[256,1024]{1,0:T(8,128)(2,1)S(1)}, u32[]{:S(2)}, u32[]{:S(2)}) collective-permute-start(bf16[256,1024]{1,0:T(8,128)(2,1)S(1)} %fusion.76), channel_id=1, source_target_pairs={{0,16},{8,24},{16,0},{24,8},{1,17},{9,25},{17,1},{25,9},{2,18},{10... | collective-permute-start | bytes 1572872 | tf_op jit(solution)/shard_map/ppermute | solution.py:213
  353.5 40.9 %collective-permute-start.16 = (bf16[256,1024]{1,0:T(8,128)(2,1)S(1)}, bf16[256,1024]{1,0:T(8,128)(2,1)S(1)}, u32[]{:S(2)}, u32[]{:S(2)}) collective-permute-start(bf16[256,1024]{1,0:T(8,128)(2,1)S(1)} %fusion.94), channel_id=1, source_target_pairs={{0,16},{8,24},{16,0},{24,8},{1,17},{9,25},{17,1},{25,9},{2,18},{10... | collective-permute-start | bytes 1572872 | tf_op jit(solution)/shard_map/ppermute | solution.py:213
  364.0 65.2 %collective-permute-start.6 = (bf16[256,1024]{1,0:T(8,128)(2,1)S(1)}, bf16[256,1024]{1,0:T(8,128)(2,1)S(1)}, u32[]{:S(2)}, u32[]{:S(2)}) collective-permute-start(bf16[256,1024]{1,0:T(8,128)(2,1)S(1)} %fusion.76), channel_id=1, source_target_pairs={{0,8},{8,0},{16,24},{24,16},{1,9},{9,1},{17,25},{25,17},{2,10},{10... | collective-permute-start | bytes 1572872 | tf_op jit(solution)/shard_map/ppermute | solution.py:213
  371.9 38.2 %collective-permute-start.15 = (bf16[256,1024]{1,0:T(8,128)(2,1)S(1)}, bf16[256,1024]{1,0:T(8,128)(2,1)S(1)}, u32[]{:S(2)}, u32[]{:S(2)}) collective-permute-start(bf16[256,1024]{1,0:T(8,128)(2,1)S(1)} %fusion.94), channel_id=1, source_target_pairs={{0,8},{8,0},{16,24},{24,16},{1,9},{9,1},{17,25},{25,17},{2,10},{10... | collective-permute-start | bytes 1572872 | tf_op jit(solution)/shard_map/ppermute | solution.py:213
  373.9 0.8 copy-start.8
  373.9 36.1 %collective-permute-start.13 = (bf16[256,1024]{1,0:T(8,128)(2,1)S(1)}, bf16[256,1024]{1,0:T(8,128)(2,1)S(1)}, u32[]{:S(2)}, u32[]{:S(2)}) collective-permute-start(bf16[256,1024]{1,0:T(8,128)(2,1)S(1)} %fusion.88), channel_id=1, source_target_pairs={{0,16},{8,24},{16,0},{24,8},{1,17},{9,25},{17,1},{25,9},{2,18},{10... | collective-permute-start | bytes 1572872 | tf_op jit(solution)/shard_map/ppermute | solution.py:213
  394.4 16.7 %collective-permute-start.17 = (bf16[256,1024]{1,0:T(8,128)(2,1)S(1)}, bf16[256,1024]{1,0:T(8,128)(2,1)S(1)}, u32[]{:S(2)}, u32[]{:S(2)}) collective-permute-start(bf16[256,1024]{1,0:T(8,128)(2,1)S(1)} %collective-permute-done.16), channel_id=1, source_target_pairs={{0,8},{8,0},{16,24},{24,16},{1,9},{9,1},{17,25},{25,17},{2,10},{10... | collective-permute-start | bytes 1572872 | tf_op jit(solution)/shard_map/ppermute | solution.py:213
  410.0 14.4 %collective-permute-start.12 = (bf16[256,1024]{1,0:T(8,128)(2,1)S(1)}, bf16[256,1024]{1,0:T(8,128)(2,1)S(1)}, u32[]{:S(2)}, u32[]{:S(2)}) collective-permute-start(bf16[256,1024]{1,0:T(8,128)(2,1)S(1)} %fusion.88), channel_id=1, source_target_pairs={{0,8},{8,0},{16,24},{24,16},{1,9},{9,1},{17,25},{25,17},{2,10},{10... | collective-permute-start | bytes 1572872 | tf_op jit(solution)/shard_map/ppermute | solution.py:213
  410.1 14.3 %collective-permute-start.10 = (bf16[256,1024]{1,0:T(8,128)(2,1)S(1)}, bf16[256,1024]{1,0:T(8,128)(2,1)S(1)}, u32[]{:S(2)}, u32[]{:S(2)}) collective-permute-start(bf16[256,1024]{1,0:T(8,128)(2,1)S(1)} %fusion.82), channel_id=1, source_target_pairs={{0,16},{8,24},{16,0},{24,8},{1,17},{9,25},{17,1},{25,9},{2,18},{10... | collective-permute-start | bytes 1572872 | tf_op jit(solution)/shard_map/ppermute | solution.py:213
  411.1 13.9 %collective-permute-start.14 = (bf16[256,1024]{1,0:T(8,128)(2,1)S(1)}, bf16[256,1024]{1,0:T(8,128)(2,1)S(1)}, u32[]{:S(2)}, u32[]{:S(2)}) collective-permute-start(bf16[256,1024]{1,0:T(8,128)(2,1)S(1)} %collective-permute-done.13), channel_id=1, source_target_pairs={{0,8},{8,0},{16,24},{24,16},{1,9},{9,1},{17,25},{25,17},{2,10},{10... | collective-permute-start | bytes 1572872 | tf_op jit(solution)/shard_map/ppermute | solution.py:213
  413.2 13.9 %collective-permute-start.9 = (bf16[256,1024]{1,0:T(8,128)(2,1)S(1)}, bf16[256,1024]{1,0:T(8,128)(2,1)S(1)}, u32[]{:S(2)}, u32[]{:S(2)}) collective-permute-start(bf16[256,1024]{1,0:T(8,128)(2,1)S(1)} %fusion.82), channel_id=1, source_target_pairs={{0,8},{8,0},{16,24},{24,16},{1,9},{9,1},{17,25},{25,17},{2,10},{10... | collective-permute-start | bytes 1572872 | tf_op jit(solution)/shard_map/ppermute | solution.py:213
  424.4 4.7 %collective-permute-start.8 = (bf16[256,1024]{1,0:T(8,128)(2,1)S(1)}, bf16[256,1024]{1,0:T(8,128)(2,1)S(1)}, u32[]{:S(2)}, u32[]{:S(2)}) collective-permute-start(bf16[256,1024]{1,0:T(8,128)(2,1)S(1)} %collective-permute-done.7), channel_id=1, source_target_pairs={{0,8},{8,0},{16,24},{24,16},{1,9},{9,1},{17,25},{25,17},{2,10},{10... | collective-permute-start | bytes 1572872 | tf_op jit(solution)/shard_map/ppermute | solution.py:213
  424.4 2.7 collective-permute-start.11
